TPU v7x, 32 devices: a whole 2x2x4 slice. The times are simulated.
32 devices in a mesh: row: 16 (over z, y, core), col: 2 (over x).
Axes of the slice: x: 2, y: 2, z: 4, core: 2. Of those that a mesh axis runs over, the one named last changes fastest.
Arguments:
- hidden: bfloat16 [4096, 768], P(('row', 'col')), may hold values from -6 to 6
- projection: bfloat16 [768, 512], replicated, may hold values from -0.21875 to 0.21875
- alpha: bfloat16 [4096], P(('row', 'col')), may hold values from -6 to 6
- probe_pairs: bfloat16 [4096, 32], P(('row', 'col')), may hold values from -6 to 6
- amplitude: float32 [1], replicated, may hold values from 0.5 to 2
- length_sq: float32 [1], replicated, may hold values from 512 to 1024
Outputs:
- grad_hidden: bfloat16 [4096, 768], P(('row', 'col'))
- grad_proj: float32 [768, 512], P('row')
All inputs are finite; a program needn't handle non-finite values.
Results may differ from a plain program's by a relative error of at most 0.023.
Values may be sent and summed in bfloat16 or wider, within the bound.
A program may use at most 64 MiB of HBM per device.

v0:
```python
import math

import jax
import jax.numpy as jnp
from jax import lax
from jax.sharding import PartitionSpec as P


def right_of(factors, probes):
    scale = 1.0 / (4 * probes)
    return jnp.concatenate(
        [
            factors[:, :1] * 0.5,
            factors[:, 1 + probes :] * -scale,
            factors[:, 1 : 1 + probes] * -scale,
        ],
        axis=1,
    )


def squares(feats):
    feat_f = feats.astype(jnp.float32)
    return jnp.sum(feat_f * feat_f, axis=1)


def per_device(hidden, projection, alpha, probe_pairs, amplitude, length_sq):
    feats = jnp.dot(hidden, projection, preferred_element_type=jnp.float32).astype(jnp.bfloat16)
    factors = jnp.concatenate([alpha[:, None], probe_pairs], axis=1)
    probes = probe_pairs.shape[1] // 2
    amp = amplitude[0]
    lsq = length_sq[0]
    width = feats.shape[1]

    def make_fold(rows_feat, rows_fac):
        rows_sq = squares(rows_feat)

        def fold(carry, pieces, start):
            cols_feat, cols_fac = pieces
            count = cols_feat.shape[0]
            size = math.gcd(count, 256)
            steps_feat = cols_feat.reshape(count // size, size, width)
            steps_fac = cols_fac.reshape(count // size, size, cols_fac.shape[1])

            def inner_step(state, blocks):
                block_feat, block_fac = blocks
                moved, rowsum = state
                block_sq = squares(block_feat)
                inner = jnp.dot(rows_feat, block_feat.T, preferred_element_type=jnp.float32)
                dist = rows_sq[:, None] + block_sq[None, :] - 2.0 * inner
                kern = amp * jnp.exp(-0.5 * dist / lsq)
                gmat = jnp.dot(
                    rows_fac, right_of(block_fac, probes).T, preferred_element_type=jnp.float32
                )
                weight = gmat * kern
                rowsum = rowsum + jnp.sum(weight, axis=1)
                moved = moved + jnp.dot(
                    weight.astype(jnp.bfloat16), block_feat, preferred_element_type=jnp.float32
                )
                return ((moved, rowsum), None)

            result, unused = lax.scan(inner_step, carry, (steps_feat, steps_fac))
            return result

        start_carry = (
            jnp.zeros((rows_feat.shape[0], width), jnp.float32),
            jnp.zeros((rows_feat.shape[0],), jnp.float32),
        )
        return (fold, start_carry)

    rows_feat, rows_fac = (
        lax.all_gather(feats, "row", axis=0, tiled=True),
        lax.all_gather(factors, "row", axis=0, tiled=True),
    )
    fold, start_carry = make_fold(rows_feat, rows_fac)
    moved, rowsum = fold(
        start_carry,
        (
            lax.all_gather(feats, "col", axis=0, tiled=True),
            lax.all_gather(factors, "col", axis=0, tiled=True),
        ),
        jnp.int32(0),
    )
    moved_own, rowsum_own = (
        lax.psum_scatter(moved, "row", scatter_dimension=0, tiled=True),
        lax.psum_scatter(rowsum, "row", scatter_dimension=0, tiled=True),
    )
    grad_feat = (2.0 / lsq * (moved_own - rowsum_own[:, None] * feats.astype(jnp.float32))).astype(
        jnp.bfloat16
    )
    grad_hidden = jnp.dot(grad_feat, projection.T, preferred_element_type=jnp.float32).astype(
        jnp.bfloat16
    )
    partial_proj = lax.dot_general(
        hidden, grad_feat, (((0,), (0,)), ((), ())), preferred_element_type=jnp.float32
    )
    share = lax.psum_scatter(
        partial_proj.astype(jnp.bfloat16), "row", scatter_dimension=0, tiled=True
    )
    grad_proj = lax.psum(share, "col").astype(jnp.float32)
    return (grad_hidden, grad_proj)


def solution(mesh):
    placed = (P(("row", "col"), None), P(), P(("row", "col")), P(("row", "col"), None), P(), P())
    return jax.shard_map(
        per_device,
        mesh=mesh,
        in_specs=placed,
        out_specs=(P(("row", "col"), None), P("row", None)),
        check_vma=False,
    )
```

profile of v0, /device:TPU:0, one launch (start us, length us, event | category | flops | bytes accessed | tf_op | source)
XLA Modules:
  0.0 210.1 jit_solution(2335286079674351256)
XLA Ops:
  7.2 1.1 copy-done
  8.3 1.9 convolution_convert_fusion.2
  11.5 0.7 pad_maximum_fusion
  12.2 5.3 %all_gather.13 = bf16[256,33]{0,1:T(8,128)(2,1)S(1)} all-gather(bf16[128,33]{0,1:T(8,128)(2,1)S(1)} %pad_maximum_fusion), channel_id=1, replica_groups=mesh['row'=16,'col'=2] {'col'}, dimensions={0}, use_global_device_ids=true | all-gather | bytes 25344 | tf_op jit(solution)/shard_map/all_gather | solution.py:79
  17.5 22.6 %all_gather.12 = bf16[2048,33]{0,1:T(8,128)(2,1)S(1)} all-gather(bf16[128,33]{0,1:T(8,128)(2,1)S(1)} %pad_maximum_fusion), channel_id=1, replica_groups=mesh['row'=16,'col'=2] {'row'}, dimensions={0}, use_global_device_ids=true | all-gather | bytes 143616 | tf_op jit(solution)/shard_map/all_gather | solution.py:72
  40.2 6.6 %all_gather.15 = bf16[256,512]{1,0:T(8,128)(2,1)S(1)} all-gather(bf16[128,512]{1,0:T(8,128)(2,1)} %convolution_convert_fusion.2), channel_id=1, replica_groups=mesh['row'=16,'col'=2] {'col'}, dimensions={0}, use_global_device_ids=true | all-gather | bytes 393216 | tf_op jit(solution)/shard_map/all_gather | solution.py:78
  46.8 0.1 multiply_reduce_fusion.1
  46.9 8.0 %all-gather.2.cloned.1.call-done = bf16[2048,512]{1,0:T(8,128)(2,1)} async-done(((bf16[128,512]{1,0:T(8,128)(2,1)}), bf16[2048,512]{1,0:T(8,128)(2,1)}) %all-gather.2.cloned.1.call-update) | async-done | bytes 2097168 | tf_op jit(solution)/shard_map/all_gather | solution.py:71
  54.9 2.2 %multiply_reduce_fusion = f32[2048]{0:T(1024)S(1)} fusion(bf16[2048,512]{1,0:T(8,128)(2,1)} %all-gather.2.cloned.1.call-done), kind=kLoop, calls=%fused_computation | loop fusion | flops 3143680 | bytes 2105344 | tf_op jit(solution)/shard_map/reduce_sum | solution.py:23
  57.2 0.9 fusion.4
  58.0 0.5 fusion.14
  58.5 2.7 %fusion.6 = f32[2048,512]{1,0:T(8,128)} fusion(bf16[256,512]{1,0:T(8,128)(2,1)S(1)} %all_gather.15, bf16[2048,256]{0,1:T(8,128)(2,1)S(1)} %get-tuple-element.29), kind=kOutput, calls=%fused_computation.12 | convolution fusion | flops 536870912 | bytes 5505024 | tf_op jit(solution)/shard_map/while/body/eval_jaxpr/dot_general | solution.py:56
  61.3 0.5 copy-done.4
  61.8 0.6 dynamic-slice.2
  63.1 32.0 %all-reduce = f32[2048]{0:T(1024)S(1)} all-reduce(f32[2048]{0:T(1024)S(1)} %get-tuple-element.28), channel_id=3, replica_groups=mesh['row'=16,'col'=2] {'row'}, use_global_device_ids=true, to_apply=%region_4.5.clone | all-reduce | flops 2048 | bytes 16384
  95.2 37.7 %reduce-scatter.5.cloned.1.call-done = f32[128,512]{1,0:T(8,128)} async-done(((f32[2048,512]{1,0:T(8,128)}), f32[128,512]{1,0:T(8,128)}) %reduce-scatter.5.cloned.1.call-update) | async-done | bytes 262160 | tf_op jit(solution)/shard_map/reduce_scatter | solution.py:84
  132.9 1.1 multiply_convert_fusion
  133.9 0.4 fusion.5
  134.3 1.2 copy.10
  135.5 1.1 convolution_convert_fusion.1
  136.6 55.7 %reduce-scatter.7.cloned.1.call-done = bf16[48,512]{1,0:T(8,128)(2,1)} async-done(((bf16[768,512]{1,0:T(8,128)(2,1)}), bf16[48,512]{1,0:T(8,128)(2,1)}) %reduce-scatter.7.cloned.1.call-update) | async-done | bytes 49168
  192.3 0.9 copy.11
  193.2 9.6 %psum.7 = bf16[48,512]{0,1:T(8,128)(2,1)S(1)} all-reduce(bf16[48,512]{0,1:T(8,128)(2,1)S(1)} %copy.11), channel_id=1, replica_groups=mesh['row'=16,'col'=2] {'col'}, use_global_device_ids=true, to_apply=%region_6.7 | all-reduce | flops 24576 | bytes 98304 | tf_op jit(solution)/shard_map/psum | solution.py:99
  202.8 0.7 copy.9
  (17 shorter events, 0.3 us)
Async XLA Ops:
  7.2 1.1 copy-start
  7.2 47.7 %all-gather.2.cloned.1.call-start = ((), (), s32[]{:S(2)}) async-start(), calls=%async_computation.2 | async-start | bytes 2228224 | tf_op jit(solution)/shard_map/all_gather | solution.py:71
  10.2 122.7 %reduce-scatter.5.cloned.1.call-start = ((), (), s32[]{:S(2)}) async-start(), calls=%async_computation.3 | async-start | bytes 4456448 | tf_op jit(solution)/shard_map/reduce_scatter | solution.py:84
  54.9 2.2 %copy-start.2 = (bf16[2048,512]{1,0:T(8,128)(2,1)S(1)}, bf16[2048,512]{1,0:T(8,128)(2,1)}, u32[]{:S(2)}) copy-start(bf16[2048,512]{1,0:T(8,128)(2,1)} %all-gather.2.cloned.1.call-done) | copy-start | bytes 6291460
  61.2 0.7 copy-start.4
  61.2 71.7 %copy-start.1 = (bf16[128,512]{1,0:T(8,128)(2,1)S(1)}, bf16[128,512]{1,0:T(8,128)(2,1)}, u32[]{:S(2)}) copy-start(bf16[128,512]{1,0:T(8,128)(2,1)} %convolution_convert_fusion.2) | copy-start | bytes 393220
  61.2 72.8 %copy-start.3 = (bf16[128,768]{1,0:T(8,128)(2,1)S(1)}, bf16[128,768]{1,0:T(8,128)(2,1)}, u32[]{:S(2)}) copy-start(bf16[128,768]{1,0:T(8,128)(2,1)} %param.6) | copy-start | bytes 589828
  61.2 131.1 %reduce-scatter.7.cloned.1.call-start = ((), (), s32[]{:S(2)}) async-start(), calls=%async_computation.4 | async-start | bytes 835584
Sparse Core Ops, SparseCore 0:
  10.7 44.1 all-gather.1
  61.3 71.4 reduce-scatter.4
  136.4 55.8 reduce-scatter.6
where the time goes:
time: 210 us
  waiting for transfers between devices  101 us (48%)
  blocking collectives  76.1 us (36%)
  between operations  15.8 us (8%)
  matrix products  7.31 us (3%)
  local copies, waits for them, and re-layouts  5.1 us (2%)
  other arithmetic  4.13 us (2%)
    unnamed x4, waiting for transfers between devices  55.8 us
    reduce_scatter x1, waiting for transfers between devices, per_device(): lax.psum_scatter(moved, 'row', scatter_dimension=0, tiled=True)  37.7 us
    unnamed x1, blocking collectives  32 us
    all_gather x1, blocking collectives, per_device(): lax.all_gather(factors, 'row', axis=0, tiled=True)  22.6 us
    psum x1, blocking collectives, per_device(): grad_proj = lax.psum(share, 'col').astype(jnp.float32)  9.58 us
    all_gather x1, waiting for transfers between devices, per_device(): lax.all_gather(feats, 'row', axis=0, tiled=True)  7.99 us
    all_gather x1, blocking collectives, per_device(): lax.all_gather(feats, 'col', axis=0, tiled=True)  6.61 us
    all_gather x1, blocking collectives, per_device(): lax.all_gather(factors, 'col', axis=0, tiled=True)  5.29 us
  transfers between devices with their start and end apart: 3, of which 3 were waited for; matrix products, arithmetic and copies ran while one was open for 1% of the time, Pallas kernels for 0%

commit v1 on v0

--- a/solution.py
+++ b/solution.py
@@ -1,8 +1,11 @@
+import functools
 import math
 
 import jax
 import jax.numpy as jnp
 from jax import lax
+from jax.experimental import pallas as pl
+from jax.experimental.pallas import tpu as pltpu
 from jax.sharding import PartitionSpec as P
 
 
@@ -100,10 +103,432 @@
     return (grad_hidden, grad_proj)
 
 
+TILE = 16
+LANES = 128
+MESH = pl.DeviceIdType.MESH
+NT = (((1,), (1,)), ((), ()))
+
+
+def fused_kernel(
+    n_q,
+    hidden,
+    proj,
+    fac,
+    amp,
+    lsq,
+    gh_ref,
+    gp_ref,
+    blocks,
+    rows_blk,
+    rows_fac,
+    rows_hid,
+    row_sq,
+    hid_t,
+    moved,
+    rowsum,
+    part_d,
+    peer_d,
+    grad,
+    y_out,
+    y_in,
+    q_out,
+    q_in,
+    x_out,
+    x_in,
+    send_sems,
+    recv_sems,
+    core_send,
+    core_recv,
+    y_send,
+    y_recv,
+    q_send,
+    q_recv,
+    x_send,
+    x_recv,
+):
+    r = lax.axis_index("row")
+    c = lax.axis_index("col")
+    k = lax.rem(r, 2)
+    y = lax.rem(r // 2, 2)
+    q = r // 4
+    pts, hid = hidden.shape
+    feat = proj.shape[1]
+    share = gp_ref.shape[0]
+    mid = pts // 2
+
+    def dev(qq, yy, cc, kk):
+        return ((qq * 2 + yy) * 2 + kk, cc)
+
+    y_nbr = dev(q, 1 - y, c, k)
+    c_nbr = dev(q, y, 1 - c, k)
+    core = dev(q, y, c, 1 - k)
+    q_up = dev(jnp.minimum(q + 1, n_q - 1), y, c, k)
+    q_dn = dev(jnp.maximum(q - 1, 0), y, c, k)
+
+    barrier = pltpu.get_barrier_semaphore()
+    for nbr in (y_nbr, c_nbr, core):
+        pl.semaphore_signal(barrier, inc=1, device_id=nbr, device_id_type=MESH)
+    for i in range(1, n_q):
+        pl.semaphore_signal(
+            barrier, inc=1, device_id=dev(lax.rem(q + i, n_q), y, c, k), device_id_type=MESH
+        )
+
+    def slot_of(oq, oy, oc):
+        return (oq * 2 + oy) * 2 + oc
+
+    mine = slot_of(q, y, c)
+
+    feats = jnp.dot(hidden[...], proj[...], preferred_element_type=jnp.float32).astype(jnp.bfloat16)
+    feat_f = feats.astype(jnp.float32)
+    sq = lax.dot_general(
+        jnp.ones((8, feat), jnp.float32),
+        feat_f * feat_f,
+        NT,
+        precision=lax.Precision.HIGHEST,
+        preferred_element_type=jnp.float32,
+    )
+    sq = jnp.concatenate([sq, sq], axis=0)
+    hi = sq.astype(jnp.bfloat16).astype(jnp.float32)
+    mi = (sq - hi).astype(jnp.bfloat16).astype(jnp.float32)
+    lo = sq - hi - mi
+    fac_t = fac[:, :LANES].astype(jnp.float32).T
+    place = lax.broadcasted_iota(jnp.int32, (TILE, pts), 0)
+    last = fac_t[2 * TILE : 3 * TILE]
+    last = jnp.where(place == 1, hi, jnp.where(place == 2, mi, jnp.where(place == 3, lo, last)))
+    blocks[mine, 0:pts, :] = feats
+    rows_blk[k] = feats
+    blocks[mine, pts:, :] = jnp.zeros((TILE, feat), jnp.bfloat16)
+    blocks[mine, pts:, 0:pts] = fac_t[0:TILE].astype(jnp.bfloat16)
+    blocks[mine, pts:, pts : 2 * pts] = fac_t[TILE : 2 * TILE].astype(jnp.bfloat16)
+    blocks[mine, pts:, 2 * pts : 3 * pts] = last.astype(jnp.bfloat16)
+    rows_fac[k] = fac[:, LANES:]
+
+    pl.semaphore_wait(barrier, 3 + n_q - 1)
+
+    def to_core(index, src, dst):
+        return pltpu.make_async_remote_copy(
+            src_ref=src,
+            dst_ref=dst,
+            send_sem=core_send.at[index],
+            recv_sem=core_recv.at[index],
+            device_id=core,
+            device_id_type=MESH,
+        )
+
+    first = (
+        to_core(0, blocks.at[mine, 0:pts], rows_blk.at[k]),
+        to_core(1, fac.at[:, LANES : 2 * LANES], rows_fac.at[k]),
+        to_core(2, hidden, rows_hid),
+    )
+
+    spans = ((0, mid), (mid, pts + TILE - mid))
+
+    def hop(direction, part, slot, nbr):
+        piece = blocks.at[slot, pl.ds(*spans[part])]
+        return pltpu.make_async_remote_copy(
+            src_ref=piece,
+            dst_ref=piece,
+            send_sem=send_sems.at[direction, part, slot],
+            recv_sem=recv_sems.at[part, slot],
+            device_id=nbr,
+            device_id_type=MESH,
+        )
+
+    sent = []
+
+    def send(pred, copy):
+        sent.append((pred, copy))
+        if pred is None:
+            copy.start()
+        else:
+            pl.when(pred)(copy.start)
+
+    def both(a, b):
+        return b if a is None else jnp.logical_and(a, b)
+
+    def forward(exists, part, oq, iy, ic, own=False):
+        slot = slot_of(oq, (y + iy) % 2, (c + ic) % 2)
+        if not own:
+            arrival = hop(0, part, slot, y_nbr)
+            pl.when(exists)(arrival.wait_recv)
+        if part == 0:
+            if iy == 0 and ic == 0:
+                send(exists, hop(3, part, slot, c_nbr))
+            if iy == 0:
+                send(exists, hop(2, part, slot, y_nbr))
+        else:
+            if iy == 0 and ic == 0:
+                send(exists, hop(2, part, slot, y_nbr))
+            if ic == 0:
+                send(exists, hop(3, part, slot, c_nbr))
+
+    def forward_q(exists, part, oq):
+        slot = slot_of(oq, y, c)
+        up = jnp.logical_and(oq <= q, q + 1 < n_q)
+        down = jnp.logical_and(oq >= q, q > 0)
+        send(both(exists, up), hop(0, part, slot, q_up))
+        send(both(exists, down), hop(1, part, slot, q_dn))
+
+    scale = -0.5 / lsq[0]
+
+    def fold(slot):
+        blk = blocks[slot, 0:pts, :]
+        aux = blocks[slot, pts:, :]
+        rows = jnp.concatenate([rows_blk[0], rows_blk[1]], axis=0)
+        inner = lax.dot_general(rows, blk, NT, preferred_element_type=jnp.float32)
+        tail = aux[:, 2 * pts : 3 * pts].astype(jnp.float32)
+        col_sq = tail[1:2] + tail[2:3] + tail[3:4]
+        dist = row_sq[...] + col_sq - 2.0 * inner
+        kern = jnp.exp(dist * scale)
+        col_fac = jnp.concatenate(
+            [
+                aux[:, 0:pts],
+                aux[:, pts : 2 * pts],
+                aux[:, 2 * pts : 3 * pts],
+                jnp.zeros((LANES - 3 * TILE, pts), jnp.bfloat16),
+            ],
+            axis=0,
+        )
+        lefts = jnp.concatenate([rows_fac[0], rows_fac[1]], axis=0)
+        gmat = jnp.dot(lefts, col_fac, preferred_element_type=jnp.float32)
+        weight = gmat * kern
+        rowsum[...] += weight
+        moved[...] += jnp.dot(weight.astype(jnp.bfloat16), blk, preferred_element_type=jnp.float32)
+
+    def fold_level(level):
+        def step(e, carry):
+            iy, ic, side = e // 4, lax.rem(e // 2, 2), lax.rem(e, 2)
+            dq = level - iy - ic
+            oq = q + dq * (1 - 2 * side)
+            good = (dq >= 0) & (dq < n_q) & (oq >= 0) & (oq < n_q) & ((dq > 0) | (side == 0))
+
+            @pl.when(good)
+            def _():
+                fold(slot_of(oq, lax.rem(y + iy, 2), lax.rem(c + ic, 2)))
+
+            return carry
+
+        lax.fori_loop(0, 8, step, 0)
+
+    for level in range(n_q + 2):
+        if level == 0:
+            for part in (0, 1):
+                forward(None, part, q, 0, 0, own=True)
+                forward_q(None, part, q)
+            for copy in first:
+                copy.start()
+            for copy in first:
+                copy.wait_recv()
+            for half in range(2):
+                f = rows_blk[half].astype(jnp.float32)
+                row_sq[half * pts : (half + 1) * pts, :] = jnp.broadcast_to(
+                    jnp.sum(f * f, axis=1, keepdims=True), (pts, pts)
+                )
+            moved[...] = jnp.zeros_like(moved)
+            rowsum[...] = jnp.zeros_like(rowsum)
+        for iy, ic in ((0, 0), (0, 1), (1, 0), (1, 1)):
+            dq = level - iy - ic
+            if dq < 0 or dq >= n_q or level == 0:
+                continue
+            for side in (1, -1) if dq else (1,):
+                oq = q + side * dq
+                exists = None if dq == 0 else jnp.logical_and(oq >= 0, oq < n_q)
+                if exists is None:
+                    exists = q >= 0
+                for part in (0, 1):
+                    forward(exists, part, oq, iy, ic)
+                    if iy == 0 and ic == 0:
+                        forward_q(exists, part, oq)
+        fold_level(level)
+        if level == 0:
+            own_t = hidden[...].astype(jnp.float32).T.astype(jnp.bfloat16)
+            peer_t = rows_hid[...].astype(jnp.float32).T.astype(jnp.bfloat16)
+            low = k == 0
+            hid_t[:, 0:pts] = jnp.where(low, own_t, peer_t)
+            hid_t[:, pts:] = jnp.where(low, peer_t, own_t)
+
+    rows_f = jnp.concatenate([rows_blk[0], rows_blk[1]], axis=0).astype(jnp.float32)
+    part_d[...] = moved[...] - jnp.sum(rowsum[...], axis=1, keepdims=True) * rows_f
+    swap = to_core(3, part_d, peer_d)
+    swap.start()
+    swap.wait_recv()
+    grad[...] = ((2.0 * amp[0] / lsq[0]) * (part_d[...] + peer_d[...])).astype(jnp.bfloat16)
+
+    def term(qj, yj):
+        start = pl.multiple_of(((qj * 2 + yj) * 2 + k) * share, TILE)
+        return jnp.dot(hid_t[pl.ds(start, share), :], grad[...], preferred_element_type=jnp.float32)
+
+    def to_y(qj):
+        return pltpu.make_async_remote_copy(
+            src_ref=y_out.at[qj],
+            dst_ref=y_in.at[qj],
+            send_sem=y_send.at[qj],
+            recv_sem=y_recv.at[qj],
+            device_id=y_nbr,
+            device_id_type=MESH,
+        )
+
+    def to_q(qj):
+        return pltpu.make_async_remote_copy(
+            src_ref=q_out.at[qj],
+            dst_ref=q_in.at[q],
+            send_sem=q_send.at[qj],
+            recv_sem=q_recv.at[q],
+            device_id=dev(qj, y, c, k),
+            device_id_type=MESH,
+        )
+
+    def from_q(qj):
+        return pltpu.make_async_remote_copy(
+            src_ref=q_out.at[qj],
+            dst_ref=q_in.at[qj],
+            send_sem=q_send.at[qj],
+            recv_sem=q_recv.at[qj],
+            device_id=dev(qj, y, c, k),
+            device_id_type=MESH,
+        )
+
+    order = [lax.rem(q + i, n_q) for i in range(1, n_q)] + [q]
+    for qj in order:
+        y_out[qj] = term(qj, 1 - y).astype(jnp.bfloat16)
+        to_y(qj).start()
+    own_rows = grad[pl.ds(pl.multiple_of(k * pts, pts), pts), :]
+    gh_ref[...] = lax.dot_general(
+        own_rows, proj[...], NT, preferred_element_type=jnp.float32
+    ).astype(jnp.bfloat16)
+    total = None
+    for qj in order:
+        own_term = term(qj, y)
+        to_y(qj).wait_recv()
+        summed = own_term + y_in[qj].astype(jnp.float32)
+        if qj is order[-1]:
+            total = summed
+        else:
+            q_out[qj] = summed.astype(jnp.bfloat16)
+            to_q(qj).start()
+    for qj in order[:-1]:
+        from_q(qj).wait_recv()
+        total = total + q_in[qj].astype(jnp.float32)
+    x_out[...] = total.astype(jnp.bfloat16)
+    to_x = pltpu.make_async_remote_copy(
+        src_ref=x_out,
+        dst_ref=x_in,
+        send_sem=x_send,
+        recv_sem=x_recv,
+        device_id=c_nbr,
+        device_id_type=MESH,
+    )
+    to_x.start()
+    to_x.wait_recv()
+    gp_ref[...] = x_out[...].astype(jnp.float32) + x_in[...].astype(jnp.float32)
+
+    for pred, copy in sent:
+        if pred is None:
+            copy.wait_send()
+        else:
+            pl.when(pred)(copy.wait_send)
+    for copy in first:
+        copy.wait_send()
+    swap.wait_send()
+    for qj in order:
+        to_y(qj).wait_send()
+    for qj in order[:-1]:
+        to_q(qj).wait_send()
+    to_x.wait_send()
+
+
+def fused(n_row, n_col, hidden, projection, alpha, probe_pairs, amplitude, length_sq):
+    pts, hid = hidden.shape
+    feat = projection.shape[1]
+    probes = probe_pairs.shape[1] // 2
+    slots = n_row * n_col // 2
+    n_q = n_row // 4
+    share = hid // n_row
+    step = 1.0 / (4 * probes)
+    fill = jnp.zeros((pts, LANES - 2 * probes - 1), jnp.bfloat16)
+    fac = jnp.concatenate(
+        [
+            probe_pairs,
+            alpha[:, None],
+            fill,
+            probe_pairs[:, probes:] * -step,
+            probe_pairs[:, :probes] * -step,
+            alpha[:, None] * 0.5,
+            fill,
+        ],
+        axis=1,
+    )
+    vmem = pl.BlockSpec(memory_space=pltpu.VMEM)
+    smem = pl.BlockSpec(memory_space=pltpu.SMEM)
+    bf, f32 = jnp.bfloat16, jnp.float32
+    dma = pltpu.SemaphoreType.DMA
+    return pl.pallas_call(
+        functools.partial(fused_kernel, n_q),
+        out_shape=(
+            jax.ShapeDtypeStruct((pts, hid), bf),
+            jax.ShapeDtypeStruct((share, feat), f32),
+        ),
+        in_specs=[vmem, vmem, vmem, smem, smem],
+        out_specs=(vmem, vmem),
+        scratch_shapes=[
+            pltpu.VMEM((slots, pts + TILE, feat), bf),
+            pltpu.VMEM((2, pts, feat), bf),
+            pltpu.VMEM((2, pts, LANES), bf),
+            pltpu.VMEM((pts, hid), bf),
+            pltpu.VMEM((2 * pts, pts), f32),
+            pltpu.VMEM((hid, 2 * pts), bf),
+            pltpu.VMEM((2 * pts, feat), f32),
+            pltpu.VMEM((2 * pts, pts), f32),
+            pltpu.VMEM((2 * pts, feat), f32),
+            pltpu.VMEM((2 * pts, feat), f32),
+            pltpu.VMEM((2 * pts, feat), bf),
+            pltpu.VMEM((n_q, share, feat), bf),
+            pltpu.VMEM((n_q, share, feat), bf),
+            pltpu.VMEM((n_q, share, feat), bf),
+            pltpu.VMEM((n_q, share, feat), bf),
+            pltpu.VMEM((share, feat), bf),
+            pltpu.VMEM((share, feat), bf),
+            dma((4, 2, slots)),
+            dma((2, slots)),
+            dma((4,)),
+            dma((4,)),
+            dma((n_q,)),
+            dma((n_q,)),
+            dma((n_q,)),
+            dma((n_q,)),
+            dma,
+            dma,
+        ],
+        compiler_params=pltpu.CompilerParams(
+            collective_id=0, has_side_effects=True, vmem_limit_bytes=32 * 1024 * 1024
+        ),
+    )(hidden, projection, fac, amplitude, length_sq)
+
+
+def per_shard(n_row, n_col, hidden, projection, alpha, probe_pairs, amplitude, length_sq):
+    pts, hid = hidden.shape
+    feat = projection.shape[1]
+    probes = probe_pairs.shape[1] // 2
+    fits = (
+        n_row % 4 == 0
+        and n_col == 2
+        and n_row * n_col <= 64
+        and pts == LANES
+        and feat % LANES == 0
+        and feat >= 3 * pts
+        and probes == TILE
+        and hid % (n_row * TILE) == 0
+    )
+    args = (hidden, projection, alpha, probe_pairs, amplitude, length_sq)
+    if fits:
+        return fused(n_row, n_col, *args)
+    return per_device(*args)
+
+
 def solution(mesh):
     placed = (P(("row", "col"), None), P(), P(("row", "col")), P(("row", "col"), None), P(), P())
     return jax.shard_map(
-        per_device,
+        functools.partial(per_shard, mesh.shape["row"], mesh.shape["col"]),
         mesh=mesh,
         in_specs=placed,
         out_specs=(P(("row", "col"), None), P("row", None)),

time: 210 us -> 50.7 us (0.24)
  waiting for transfers between devices: 101 us -> 0 us
  blocking collectives: 76.1 us -> 0 us
  Pallas kernels: 0 us -> 43.3 us
  between operations: 15.8 us -> 1.96 us
  matrix products: 7.31 us -> 0 us
  other arithmetic: 4.13 us -> 0.71 us
    unnamed x4 -> x0, waiting for transfers between devices: 55.8 us -> none
    pallas_call x0 -> x1, Pallas kernels: none -> 43.3 us  [fused(): pl.pallas_call(functools.partial(fused_kernel, n_q), out_shape=(jax.Shape...]
    reduce_scatter x1 -> x0, waiting for transfers between devices: 37.7 us -> none  [per_device(): lax.psum_scatter(moved, 'row', scatter_dimension=0, tiled=True)]
    all_gather x3 -> x0, blocking collectives: 34.5 us -> none  [the longest x1 22.6 us: per_device(): lax.all_gather(factors, 'row', axis=0, tiled=True)]
    unnamed x1 -> x0, blocking collectives: 32 us -> none
    psum x1 -> x0, blocking collectives: 9.58 us -> none  [per_device(): grad_proj = lax.psum(share, 'col').astype(jnp.float32)]
    all_gather x1 -> x0, waiting for transfers between devices: 7.99 us -> none  [per_device(): lax.all_gather(feats, 'row', axis=0, tiled=True)]
    dot_general x6 -> x0, matrix products: 7.31 us -> none  [the longest x1 2.67 us: inner_step(): jnp.dot(weight.astype(jnp.bfloat16), block_feat, preferred_element_type=j...]
  transfers between devices with their start and end apart: 3 -> 0, of which waited for: 3 -> 0; matrix products, arithmetic and copies ran while one was open for 1% -> 0% of each run, Pallas kernels for 0% -> 0%
where the time goes in v1:
time: 50.7 us; the launch traced here: 50.4 us
  Pallas kernels  43.3 us (85%)
  local copies, waits for them, and re-layouts  4.4 us (9%)
  between operations  1.96 us (4%)
  other arithmetic  0.71 us (1%)
    pallas_call x1, Pallas kernels, fused(): pl.pallas_call(functools.partial(fused_kernel, n_q), out_shape=(jax.Shape...  43.3 us
    unnamed x11, local copies, waits for them, and re-layouts  3.74 us

profile of v1, /device:TPU:0, one launch (start us, length us, event | category | flops | bytes accessed | tf_op | source)
XLA Modules:
  0.0 50.4 jit_solution(12716221645354431131)
XLA Ops:
  1.9 0.0 copy-start.3
  1.9 0.6 %copy-done.3 = bf16[128]{0:T(256)(128)(2,1)S(1)} copy-done((bf16[128]{0:T(256)(128)(2,1)S(1)}, bf16[128]{0:T(256)(128)(2,1)}, u32[]{:S(2)}) %copy-start.3) | copy-done | bytes 280
  2.6 0.7 %slice_multiply_fusion = (bf16[128,16]{0,1:T(8,128)(2,1)S(1)}, bf16[128,16]{0,1:T(8,128)(2,1)S(1)}) fusion(bf16[128,32]{0,1:T(8,128)(2,1)} %param.9), kind=kLoop, calls=%fused_computation | loop fusion | flops 4096 | bytes 16384 | tf_op jit(solution)/shard_map/mul | solution.py:455
  3.3 0.1 copy.18
  3.4 0.1 copy.19
  3.6 0.0 copy-start.2
  3.6 0.1 copy.17
  3.7 0.0 copy-start.1
  3.7 0.1 copy.16
  3.8 0.4 copy-done.2
  4.3 0.1 copy.15
  4.4 0.1 concatenate.3.fac
  4.5 0.1 copy-done.1
  4.6 0.0 copy-start
  4.6 1.1 %copy-done = bf16[768,512]{1,0:T(8,128)(2,1)S(1)} copy-done((bf16[768,512]{1,0:T(8,128)(2,1)S(1)}, bf16[768,512]{1,0:T(8,128)(2,1)}, u32[]{:S(2)}) %copy-start) | copy-done | bytes 786456
  5.7 43.3 %shard_map.77 = (bf16[128,768]{1,0:T(8,128)(2,1)S(1)}, f32[48,512]{1,0:T(8,128)S(1)}) custom-call(bf16[128,768]{1,0:T(8,128)(2,1)S(1)} %copy-done.1, bf16[768,512]{1,0:T(8,128)(2,1)S(1)} %copy-done, bf16[128,256]{1,0:T(8,128)(2,1)S(1)} %concatenate.3.fac, f32[1]{0:T(128)S(6)} %copy.22.amp, f32[1]{0:T(128)S(6)} %copy.23.lsq), custom_call_target="tpu_custom_call" | custom-call | tf_op jit(solution)/shard_map/pallas_call | solution.py:465
  49.1 0.7 %copy.24 = bf16[128,768]{1,0:T(8,128)(2,1)} copy(bf16[128,768]{1,0:T(8,128)(2,1)S(1)} %get-tuple-element.6) | data formatting | bytes 393216
  49.7 0.6 %copy.25 = f32[48,512]{1,0:T(8,128)} copy(f32[48,512]{1,0:T(8,128)S(1)} %get-tuple-element.7) | data formatting | bytes 196608
  (2 shorter events, 0.0 us)
Async XLA Ops:
  1.9 0.7 %copy-start.3 = (bf16[128]{0:T(256)(128)(2,1)S(1)}, bf16[128]{0:T(256)(128)(2,1)}, u32[]{:S(2)}) copy-start(bf16[128]{0:T(256)(128)(2,1)} %param.8) | copy-start | bytes 772
  3.6 0.7 %copy-start.2 = (bf16[128,32]{0,1:T(8,128)(2,1)S(1)}, bf16[128,32]{0,1:T(8,128)(2,1)}, u32[]{:S(2)}) copy-start(bf16[128,32]{0,1:T(8,128)(2,1)} %param.9) | copy-start | bytes 24580
  3.7 0.9 %copy-start.1 = (bf16[128,768]{1,0:T(8,128)(2,1)S(1)}, bf16[128,768]{1,0:T(8,128)(2,1)}, u32[]{:S(2)}) copy-start(bf16[128,768]{1,0:T(8,128)(2,1)} %hidden.1) | copy-start | bytes 589828
  4.6 1.1 %copy-start = (bf16[768,512]{1,0:T(8,128)(2,1)S(1)}, bf16[768,512]{1,0:T(8,128)(2,1)}, u32[]{:S(2)}) copy-start(bf16[768,512]{1,0:T(8,128)(2,1)} %proj.1) | copy-start | bytes 2359300

commit v2 on v1

--- a/solution.py
+++ b/solution.py
@@ -105,15 +105,18 @@
 
 TILE = 16
 LANES = 128
+ROUTES = ("qcy", "qyc", "ycq")
+FIRST_SENDS = ("2y", "0c", "0q", "1q", "1y", "2c", "0y", "1c", "2q")
 MESH = pl.DeviceIdType.MESH
 NT = (((1,), (1,)), ((), ()))
 
 
 def fused_kernel(
     n_q,
-    hidden,
-    proj,
-    fac,
+    hidden_hbm,
+    proj_hbm,
+    pairs_hbm,
+    alpha_ref,
     amp,
     lsq,
     gh_ref,
@@ -122,6 +125,9 @@
     rows_blk,
     rows_fac,
     rows_hid,
+    hidden,
+    proj,
+    pairs,
     row_sq,
     hid_t,
     moved,
@@ -145,7 +151,16 @@
     q_recv,
     x_send,
     x_recv,
+    load_sems,
 ):
+    loads = [
+        pltpu.make_async_copy(src, dst, load_sems.at[i])
+        for i, (src, dst) in enumerate(
+            ((proj_hbm, proj), (hidden_hbm, hidden), (pairs_hbm, pairs))
+        )
+    ]
+    for load in loads:
+        load.start()
     r = lax.axis_index("row")
     c = lax.axis_index("col")
     k = lax.rem(r, 2)
@@ -154,7 +169,8 @@
     pts, hid = hidden.shape
     feat = proj.shape[1]
     share = gp_ref.shape[0]
-    mid = pts // 2
+    probes = pairs.shape[1] // 2
+    step_scale = 1.0 / (4 * probes)
 
     def dev(qq, yy, cc, kk):
         return ((qq * 2 + yy) * 2 + kk, cc)
@@ -177,6 +193,9 @@
         return (oq * 2 + oy) * 2 + oc
 
     mine = slot_of(q, y, c)
+
+    for load in loads:
+        load.wait()
 
     feats = jnp.dot(hidden[...], proj[...], preferred_element_type=jnp.float32).astype(jnp.bfloat16)
     feat_f = feats.astype(jnp.float32)
@@ -191,17 +210,20 @@
     hi = sq.astype(jnp.bfloat16).astype(jnp.float32)
     mi = (sq - hi).astype(jnp.bfloat16).astype(jnp.float32)
     lo = sq - hi - mi
-    fac_t = fac[:, :LANES].astype(jnp.float32).T
+    eye = lax.broadcasted_iota(jnp.int32, (2 * probes, 2 * probes), 0)
+    eye = (eye == lax.broadcasted_iota(jnp.int32, (2 * probes, 2 * probes), 1)).astype(jnp.bfloat16)
+    pairs_t = lax.dot_general(eye, pairs[...], NT, preferred_element_type=jnp.float32)
     place = lax.broadcasted_iota(jnp.int32, (TILE, pts), 0)
-    last = fac_t[2 * TILE : 3 * TILE]
+    last = jnp.where(
+        place == 0, jnp.broadcast_to(alpha_ref[...].astype(jnp.float32), (TILE, pts)), 0.0
+    )
     last = jnp.where(place == 1, hi, jnp.where(place == 2, mi, jnp.where(place == 3, lo, last)))
     blocks[mine, 0:pts, :] = feats
-    rows_blk[k] = feats
-    blocks[mine, pts:, :] = jnp.zeros((TILE, feat), jnp.bfloat16)
-    blocks[mine, pts:, 0:pts] = fac_t[0:TILE].astype(jnp.bfloat16)
-    blocks[mine, pts:, pts : 2 * pts] = fac_t[TILE : 2 * TILE].astype(jnp.bfloat16)
+    blocks[mine, pts:, 3 * pts :] = jnp.zeros((TILE, feat - 3 * pts), jnp.bfloat16)
+    blocks[mine, pts:, 0:pts] = pairs_t[0:TILE].astype(jnp.bfloat16)
+    blocks[mine, pts:, pts : 2 * pts] = pairs_t[TILE : 2 * TILE].astype(jnp.bfloat16)
     blocks[mine, pts:, 2 * pts : 3 * pts] = last.astype(jnp.bfloat16)
-    rows_fac[k] = fac[:, LANES:]
+    rows_blk[k] = blocks[mine]
 
     pl.semaphore_wait(barrier, 3 + n_q - 1)
 
@@ -215,13 +237,10 @@
             device_id_type=MESH,
         )
 
-    first = (
-        to_core(0, blocks.at[mine, 0:pts], rows_blk.at[k]),
-        to_core(1, fac.at[:, LANES : 2 * LANES], rows_fac.at[k]),
-        to_core(2, hidden, rows_hid),
-    )
-
-    spans = ((0, mid), (mid, pts + TILE - mid))
+    first = (to_core(0, blocks.at[mine], rows_blk.at[k]), to_core(2, hidden, rows_hid))
+
+    cut = (pts // 4, 5 * pts // 8)
+    spans = ((cut[1], pts + TILE - cut[1]), (cut[0], cut[1] - cut[0]), (0, cut[0]))
 
     def hop(direction, part, slot, nbr):
         piece = blocks.at[slot, pl.ds(*spans[part])]
@@ -246,35 +265,33 @@
     def both(a, b):
         return b if a is None else jnp.logical_and(a, b)
 
-    def forward(exists, part, oq, iy, ic, own=False):
+    def send_along(dim, exists, part, oq, slot):
+        if dim == "y":
+            send(exists, hop(2, part, slot, y_nbr))
+        elif dim == "c":
+            send(exists, hop(3, part, slot, c_nbr))
+        else:
+            up = jnp.logical_and(oq <= q, q + 1 < n_q)
+            down = jnp.logical_and(oq >= q, q > 0)
+            send(both(exists, up), hop(0, part, slot, q_up))
+            send(both(exists, down), hop(1, part, slot, q_dn))
+
+    def forward(exists, part, oq, dq, iy, ic):
         slot = slot_of(oq, (y + iy) % 2, (c + ic) % 2)
-        if not own:
-            arrival = hop(0, part, slot, y_nbr)
-            pl.when(exists)(arrival.wait_recv)
-        if part == 0:
-            if iy == 0 and ic == 0:
-                send(exists, hop(3, part, slot, c_nbr))
-            if iy == 0:
-                send(exists, hop(2, part, slot, y_nbr))
-        else:
-            if iy == 0 and ic == 0:
-                send(exists, hop(2, part, slot, y_nbr))
-            if ic == 0:
-                send(exists, hop(3, part, slot, c_nbr))
-
-    def forward_q(exists, part, oq):
-        slot = slot_of(oq, y, c)
-        up = jnp.logical_and(oq <= q, q + 1 < n_q)
-        down = jnp.logical_and(oq >= q, q > 0)
-        send(both(exists, up), hop(0, part, slot, q_up))
-        send(both(exists, down), hop(1, part, slot, q_dn))
+        pl.when(exists)(hop(0, part, slot, y_nbr).wait_recv)
+        apart = {"q": dq, "y": iy, "c": ic}
+        route = ROUTES[part]
+        latest = max(at for at, dim in enumerate(route) if apart[dim])
+        for at, dim in enumerate(route):
+            if at > latest or (at == latest and dim == "q"):
+                send_along(dim, exists, part, oq, slot)
 
     scale = -0.5 / lsq[0]
 
     def fold(slot):
         blk = blocks[slot, 0:pts, :]
         aux = blocks[slot, pts:, :]
-        rows = jnp.concatenate([rows_blk[0], rows_blk[1]], axis=0)
+        rows = jnp.concatenate([rows_blk[0, 0:pts], rows_blk[1, 0:pts]], axis=0)
         inner = lax.dot_general(rows, blk, NT, preferred_element_type=jnp.float32)
         tail = aux[:, 2 * pts : 3 * pts].astype(jnp.float32)
         col_sq = tail[1:2] + tail[2:3] + tail[3:4]
@@ -289,7 +306,7 @@
             ],
             axis=0,
         )
-        lefts = jnp.concatenate([rows_fac[0], rows_fac[1]], axis=0)
+        lefts = rows_fac[...]
         gmat = jnp.dot(lefts, col_fac, preferred_element_type=jnp.float32)
         weight = gmat * kern
         rowsum[...] += weight
@@ -310,44 +327,55 @@
 
         lax.fori_loop(0, 8, step, 0)
 
-    for level in range(n_q + 2):
-        if level == 0:
-            for part in (0, 1):
-                forward(None, part, q, 0, 0, own=True)
-                forward_q(None, part, q)
-            for copy in first:
-                copy.start()
-            for copy in first:
-                copy.wait_recv()
-            for half in range(2):
-                f = rows_blk[half].astype(jnp.float32)
-                row_sq[half * pts : (half + 1) * pts, :] = jnp.broadcast_to(
-                    jnp.sum(f * f, axis=1, keepdims=True), (pts, pts)
-                )
-            moved[...] = jnp.zeros_like(moved)
-            rowsum[...] = jnp.zeros_like(rowsum)
+    def arrivals(level):
         for iy, ic in ((0, 0), (0, 1), (1, 0), (1, 1)):
             dq = level - iy - ic
-            if dq < 0 or dq >= n_q or level == 0:
+            if dq < 0 or dq >= n_q:
                 continue
             for side in (1, -1) if dq else (1,):
                 oq = q + side * dq
-                exists = None if dq == 0 else jnp.logical_and(oq >= 0, oq < n_q)
-                if exists is None:
-                    exists = q >= 0
-                for part in (0, 1):
-                    forward(exists, part, oq, iy, ic)
-                    if iy == 0 and ic == 0:
-                        forward_q(exists, part, oq)
-        fold_level(level)
-        if level == 0:
+                exists = jnp.logical_and(oq >= 0, oq < n_q)
+                for part in range(len(ROUTES)):
+                    forward(exists, part, oq, dq, iy, ic)
+
+    for first_send in FIRST_SENDS:
+        send_along(first_send[1], None, int(first_send[0]), q, mine)
+    for copy in first:
+        copy.start()
+    moved[...] = jnp.zeros_like(moved)
+    rowsum[...] = jnp.zeros_like(rowsum)
+    for copy in first:
+        copy.wait_recv()
+    for half in range(2):
+        f = rows_blk[half, 0:pts].astype(jnp.float32)
+        span = slice(half * pts, (half + 1) * pts)
+        row_sq[span, :] = jnp.broadcast_to(jnp.sum(f * f, axis=1, keepdims=True), (pts, pts))
+        aux = rows_blk[half, pts:, 0 : 3 * pts].astype(jnp.float32)
+        left_t = jnp.concatenate(
+            [
+                aux[:, pts : 2 * pts] * -step_scale,
+                aux[:, 0:pts] * -step_scale,
+                jnp.where(place == 0, aux[:, 2 * pts :] * 0.5, 0.0),
+                jnp.zeros((LANES - 3 * TILE, pts), jnp.float32),
+            ],
+            axis=0,
+        )
+        rows_fac[span, :] = left_t.T.astype(jnp.bfloat16)
+
+    for level in range(n_q + 2):
+        if level + 1 < n_q + 1:
+            arrivals(level + 1)
+        if level == n_q + 1:
+            arrivals(level)
+        if level == 1:
             own_t = hidden[...].astype(jnp.float32).T.astype(jnp.bfloat16)
             peer_t = rows_hid[...].astype(jnp.float32).T.astype(jnp.bfloat16)
             low = k == 0
             hid_t[:, 0:pts] = jnp.where(low, own_t, peer_t)
             hid_t[:, pts:] = jnp.where(low, peer_t, own_t)
-
-    rows_f = jnp.concatenate([rows_blk[0], rows_blk[1]], axis=0).astype(jnp.float32)
+        fold_level(level)
+
+    rows_f = jnp.concatenate([rows_blk[0, 0:pts], rows_blk[1, 0:pts]], axis=0).astype(jnp.float32)
     part_d[...] = moved[...] - jnp.sum(rowsum[...], axis=1, keepdims=True) * rows_f
     swap = to_core(3, part_d, peer_d)
     swap.start()
@@ -388,7 +416,12 @@
             device_id_type=MESH,
         )
 
-    order = [lax.rem(q + i, n_q) for i in range(1, n_q)] + [q]
+    order = []
+    for i in range(n_q - 1):
+        rising = jnp.where(i >= q, i + 1, i)
+        falling = jnp.where(n_q - 1 - i <= q, n_q - 2 - i, n_q - 1 - i)
+        order.append(jnp.where(2 * q < n_q, falling, rising))
+    order.append(q)
     for qj in order:
         y_out[qj] = term(qj, 1 - y).astype(jnp.bfloat16)
         to_y(qj).start()
@@ -444,21 +477,8 @@
     slots = n_row * n_col // 2
     n_q = n_row // 4
     share = hid // n_row
-    step = 1.0 / (4 * probes)
-    fill = jnp.zeros((pts, LANES - 2 * probes - 1), jnp.bfloat16)
-    fac = jnp.concatenate(
-        [
-            probe_pairs,
-            alpha[:, None],
-            fill,
-            probe_pairs[:, probes:] * -step,
-            probe_pairs[:, :probes] * -step,
-            alpha[:, None] * 0.5,
-            fill,
-        ],
-        axis=1,
-    )
     vmem = pl.BlockSpec(memory_space=pltpu.VMEM)
+    hbm = pl.BlockSpec(memory_space=pl.ANY)
     smem = pl.BlockSpec(memory_space=pltpu.SMEM)
     bf, f32 = jnp.bfloat16, jnp.float32
     dma = pltpu.SemaphoreType.DMA
@@ -468,13 +488,16 @@
             jax.ShapeDtypeStruct((pts, hid), bf),
             jax.ShapeDtypeStruct((share, feat), f32),
         ),
-        in_specs=[vmem, vmem, vmem, smem, smem],
+        in_specs=[hbm, hbm, hbm, vmem, smem, smem],
         out_specs=(vmem, vmem),
         scratch_shapes=[
             pltpu.VMEM((slots, pts + TILE, feat), bf),
-            pltpu.VMEM((2, pts, feat), bf),
-            pltpu.VMEM((2, pts, LANES), bf),
+            pltpu.VMEM((2, pts + TILE, feat), bf),
+            pltpu.VMEM((2 * pts, LANES), bf),
             pltpu.VMEM((pts, hid), bf),
+            pltpu.VMEM((pts, hid), bf),
+            pltpu.VMEM((hid, feat), bf),
+            pltpu.VMEM((pts, 2 * probes), bf),
             pltpu.VMEM((2 * pts, pts), f32),
             pltpu.VMEM((hid, 2 * pts), bf),
             pltpu.VMEM((2 * pts, feat), f32),
@@ -488,8 +511,8 @@
             pltpu.VMEM((n_q, share, feat), bf),
             pltpu.VMEM((share, feat), bf),
             pltpu.VMEM((share, feat), bf),
-            dma((4, 2, slots)),
-            dma((2, slots)),
+            dma((4, len(ROUTES), slots)),
+            dma((len(ROUTES), slots)),
             dma((4,)),
             dma((4,)),
             dma((n_q,)),
@@ -498,11 +521,12 @@
             dma((n_q,)),
             dma,
             dma,
+            dma((3,)),
         ],
         compiler_params=pltpu.CompilerParams(
             collective_id=0, has_side_effects=True, vmem_limit_bytes=32 * 1024 * 1024
         ),
-    )(hidden, projection, fac, amplitude, length_sq)
+    )(hidden, projection, probe_pairs, alpha[None, :], amplitude, length_sq)
 
 
 def per_shard(n_row, n_col, hidden, projection, alpha, probe_pairs, amplitude, length_sq):

time: 50.7 us -> 50.5 us (level)
  Pallas kernels: 43.3 us -> 44.2 us
  other arithmetic: 0.71 us -> 0 us
    pallas_call x1, Pallas kernels: 43.3 us -> 44.2 us  [fused(): pl.pallas_call(functools.partial(fused_kernel, n_q), out_shape=(jax.Shape...]
    mul x2 -> x0, other arithmetic: 0.71 us -> none  [the longest x1 0.71 us: fused(): probe_pairs[:, :probes] * -step]
    unnamed x11 -> x9, local copies, waits for them, and re-layouts: 3.74 us -> 4.2 us
where the time goes in v2:
time: 50.5 us; the launch traced here: 50.3 us
  Pallas kernels  44.2 us (88%)
  local copies, waits for them, and re-layouts  4.2 us (8%)
  between operations  1.95 us (4%)
    pallas_call x1, Pallas kernels, fused(): pl.pallas_call(functools.partial(fused_kernel, n_q), out_shape=(jax.Shape...  44.2 us
    unnamed x9, local copies, waits for them, and re-layouts  4.2 us

profile of v2, /device:TPU:0, one launch (start us, length us, event | category | flops | bytes accessed | tf_op | source)
XLA Modules:
  0.0 50.3 jit_solution(14953455278364364562)
XLA Ops:
  1.9 0.0 copy-start.2
  1.9 0.8 %copy.8.pairs_hbm = bf16[128,32]{1,0:T(8,128)(2,1)S(1)} copy(bf16[128,32]{0,1:T(8,128)(2,1)} %param.9) | data formatting | bytes 16384 | tf_op args[3]
  2.7 0.0 copy-done.2
  2.8 0.0 copy-start
  2.8 1.1 %copy-done = bf16[768,512]{1,0:T(8,128)(2,1)S(1)} copy-done((bf16[768,512]{1,0:T(8,128)(2,1)S(1)}, bf16[768,512]{1,0:T(8,128)(2,1)}, u32[]{:S(2)}) %copy-start) | copy-done | bytes 786456
  3.9 0.0 copy-start.1
  3.9 0.9 %copy-done.1 = bf16[128,768]{1,0:T(8,128)(2,1)S(1)} copy-done((bf16[128,768]{1,0:T(8,128)(2,1)S(1)}, bf16[128,768]{1,0:T(8,128)(2,1)}, u32[]{:S(2)}) %copy-start.1) | copy-done | bytes 196632
  4.8 44.2 %shard_map.77 = (bf16[128,768]{1,0:T(8,128)(2,1)S(1)}, f32[48,512]{1,0:T(8,128)S(1)}) custom-call(bf16[128,768]{1,0:T(8,128)(2,1)S(1)} %copy-done.1, bf16[768,512]{1,0:T(8,128)(2,1)S(1)} %copy-done, bf16[128,32]{1,0:T(8,128)(2,1)S(1)} %copy.8.pairs_hbm, bf16[1,128]{1,0:T(2,128)(2,1)S(1)} %bitcast.1, f32[1]{0:T(128)S(6)} %copy.11.amp, f32[1]{0:T(128)S(6)} %copy.12.lsq), custom_call_target="tpu_custom_call" | custom-call | tf_op jit(solution)/shard_map/pallas_call | solution.py:485
  49.0 0.7 %copy.13 = bf16[128,768]{1,0:T(8,128)(2,1)} copy(bf16[128,768]{1,0:T(8,128)(2,1)S(1)} %get-tuple-element.4) | data formatting | bytes 393216
  49.7 0.6 %copy.14 = f32[48,512]{1,0:T(8,128)} copy(f32[48,512]{1,0:T(8,128)S(1)} %get-tuple-element.5) | data formatting | bytes 196608
Async XLA Ops:
  1.9 0.8 %copy-start.2 = (bf16[128]{0:T(256)(128)(2,1)S(1)}, bf16[128]{0:T(256)(128)(2,1)}, u32[]{:S(2)}) copy-start(bf16[128]{0:T(256)(128)(2,1)} %param.8) | copy-start | bytes 772
  2.8 1.1 %copy-start = (bf16[768,512]{1,0:T(8,128)(2,1)S(1)}, bf16[768,512]{1,0:T(8,128)(2,1)}, u32[]{:S(2)}) copy-start(bf16[768,512]{1,0:T(8,128)(2,1)} %proj_hbm.1) | copy-start | bytes 2359300
  3.9 0.9 %copy-start.1 = (bf16[128,768]{1,0:T(8,128)(2,1)S(1)}, bf16[128,768]{1,0:T(8,128)(2,1)}, u32[]{:S(2)}) copy-start(bf16[128,768]{1,0:T(8,128)(2,1)} %hidden_hbm.1) | copy-start | bytes 589828

commit v3 on v2

--- a/solution.py
+++ b/solution.py
@@ -363,9 +363,7 @@
         rows_fac[span, :] = left_t.T.astype(jnp.bfloat16)
 
     for level in range(n_q + 2):
-        if level + 1 < n_q + 1:
-            arrivals(level + 1)
-        if level == n_q + 1:
+        if level > 0:
             arrivals(level)
         if level == 1:
             own_t = hidden[...].astype(jnp.float32).T.astype(jnp.bfloat16)
@@ -524,7 +522,7 @@
             dma((3,)),
         ],
         compiler_params=pltpu.CompilerParams(
-            collective_id=0, has_side_effects=True, vmem_limit_bytes=32 * 1024 * 1024
+            collective_id=0, has_side_effects=True, vmem_limit_bytes=62 * 1024 * 1024
         ),
     )(hidden, projection, probe_pairs, alpha[None, :], amplitude, length_sq)
 

time: 50.5 us -> 49.6 us (0.982)
    unnamed x9 -> x5, local copies, waits for them, and re-layouts: 4.2 us -> 3.71 us
where the time goes in v3:
time: 49.6 us; the launch traced here: 49.3 us
  Pallas kernels  43.7 us (88%)
  local copies, waits for them, and re-layouts  3.71 us (7%)
  between operations  1.94 us (4%)
    pallas_call x1, Pallas kernels, fused(): pl.pallas_call(functools.partial(fused_kernel, n_q), out_shape=(jax.Shape...  43.7 us
    unnamed x5, local copies, waits for them, and re-layouts  3.71 us

profile of v3, /device:TPU:0, one launch (start us, length us, event | category | flops | bytes accessed | tf_op | source)
XLA Modules:
  0.0 49.3 jit_solution(13421812444484945223)
XLA Ops:
  1.9 1.4 %copy.8.pairs_hbm = bf16[128,32]{1,0:T(8,128)(2,1)} copy(bf16[128,32]{0,1:T(8,128)(2,1)} %param.9) | data formatting | bytes 16384 | tf_op args[3]
  3.3 43.7 %shard_map.77 = (bf16[128,768]{1,0:T(8,128)(2,1)}, f32[48,512]{1,0:T(8,128)}) custom-call(bf16[128,768]{1,0:T(8,128)(2,1)} %hidden_hbm.1, bf16[768,512]{1,0:T(8,128)(2,1)} %proj_hbm.1, bf16[128,32]{1,0:T(8,128)(2,1)} %copy.8.pairs_hbm, bf16[1,128]{1,0:T(2,128)(2,1)} %bitcast.1, f32[1]{0:T(128)S(6)} %copy.11.amp, f32[1]{0:T(128)S(6)} %copy.12.lsq), custom_call_target="tpu_custom_call" | custom-call | tf_op jit(solution)/shard_map/pallas_call | solution.py:483
  47.0 0.0 copy-start
  47.0 1.6 %copy.13 = bf16[128,768]{1,0:T(8,128)(2,1)} copy(bf16[128,768]{1,0:T(8,128)(2,1)} %get-tuple-element.4) | data formatting | bytes 393216
  48.7 0.0 copy-done
  48.7 0.6 %copy.14 = f32[48,512]{1,0:T(8,128)} copy(f32[48,512]{1,0:T(8,128)S(1)} %copy-done) | data formatting | bytes 196608
Async XLA Ops:
  47.0 1.7 %copy-start = (f32[48,512]{1,0:T(8,128)S(1)}, f32[48,512]{1,0:T(8,128)}, u32[]{:S(2)}) copy-start(f32[48,512]{1,0:T(8,128)} %get-tuple-element.5) | copy-start | bytes 294916
